TPU v7x, 32 devices: a whole 2x2x4 slice. The times are simulated.
32 devices in a mesh: sfc: 8 (over z, y), sub: 4 (over x, core).
Axes of the slice: x: 2, y: 2, z: 4, core: 2. Of those that a mesh axis runs over, the one named last changes fastest.
Arguments:
- vectors: float32 [64, 512, 256], P(None, ('sfc', 'sub')), may hold values from -10 to 10
- reaction: float32 [512, 256], P(('sfc', 'sub')), may hold values from 0.5 to 5
Outputs:
- basis: float32 [64, 512, 256], P(None, ('sfc', 'sub'))
- upper: float32 [64, 64], replicated
All inputs are finite; a program needn't handle non-finite values.
Results may differ from a plain program's by a relative error of at most 0.0003.
Values sent between devices are 32-bit elements; how exact they have to be, the bound alone decides.
A program may use at most 64 MiB of HBM per device.

v0:
```python
import math
import jax
import jax.numpy as jnp
from jax import lax
from jax.sharding import PartitionSpec as P

NY = 32
NL = 8
POWERS = 3
DELTA_MASS = 0.5


def with_halo(cells, sides, width):
    for axis, dim in sides:
        count = lax.axis_size(axis)
        ends = count - 1
        head = lax.slice_in_dim(cells, 0, width, axis=dim)
        tail = lax.slice_in_dim(cells, cells.shape[dim] - width, cells.shape[dim], axis=dim)
        cells = jnp.concatenate(
            [
                lax.ppermute(tail, axis, [(i, (i + 1) % count) for i in range(ends)]),
                cells,
                lax.ppermute(head, axis, [((i + 1) % count, i) for i in range(ends)]),
            ],
            axis=dim,
        )
    return cells


def line_tables(count):
    index = jnp.arange(count)
    offset = index[:, None] - index[None, :]
    near = (jnp.abs(offset) == 1).astype(jnp.float32)
    same = (offset == 0).astype(jnp.float32)
    mass = (4.0 * same + near) / 6.0
    stiff = 2.0 * same - near
    return (mass, stiff)


def tables(across, layers):
    mass_across, stiff_across = line_tables(across)
    mass_layers, stiff_layers = line_tables(layers)
    mass_plane = jnp.kron(mass_layers, mass_across)
    stiff_plane = (
        jnp.kron(mass_layers, stiff_across)
        + jnp.kron(stiff_layers, mass_across)
        + DELTA_MASS * mass_plane
    )
    return jnp.concatenate([mass_plane, stiff_plane], axis=1)


def plane_products(field, table):
    plane = table.shape[0]
    both = jnp.einsum("kzp,pq->kzq", field, table, precision=lax.Precision.HIGHEST)
    return (both[..., :plane], both[..., plane:])


def operate(field, reaction, table):
    massed, mixed = plane_products(field, table)
    edge_term = mixed / 6.0 - massed
    padded = with_halo(edge_term, ((("sfc", "sub"), 1),), 1)
    neighbours = padded[:, :-2] + padded[:, 2:]
    return neighbours + 4.0 / 6.0 * mixed + 2.0 * massed + reaction[None] * field


def whole_factor(local):
    gram = jnp.dot(local, local.T, precision=lax.Precision.HIGHEST)
    total = lax.psum(gram, ("sfc", "sub"))
    return jnp.linalg.cholesky(total)


def lower_solve(lower, block):
    return lax.linalg.triangular_solve(lower, block, left_side=True, lower=True)


def per_device(vectors, reaction):
    table = tables(NY, NL)
    field = vectors
    for _ in range(POWERS):
        field = operate(field, reaction, table)
    local = field.reshape(field.shape[0], -1)
    lower_one = whole_factor(local)
    first = lower_solve(lower_one, local)
    lower_two = whole_factor(first)
    second = lower_solve(lower_two, first)
    scale = math.sqrt(lax.axis_size("sfc") * lax.axis_size("sub") * local.shape[1])
    upper = jnp.dot(lower_one, lower_two, precision=lax.Precision.HIGHEST).T / scale
    return ((second * scale).reshape(vectors.shape), upper)


def solution(mesh):
    placed = (P(None, ("sfc", "sub"), None), P(("sfc", "sub"), None))
    return jax.shard_map(
        per_device,
        mesh=mesh,
        in_specs=placed,
        out_specs=(P(None, ("sfc", "sub"), None), P()),
        check_vma=False,
    )
```

profile of v0, /device:TPU:0, one launch (start us, length us, event | category | flops | bytes accessed | tf_op | source)
XLA Modules:
  0.0 152.5 jit_solution(1561632378919360733)
XLA Ops:
  1.6 0.5 copy-done
  2.2 2.3 %convolution_bitcast_fusion = f32[64,16,512]{2,0,1:T(8,128)S(1)} fusion(f32[64,16,256]{2,1,0:T(8,128)S(1)} %copy-done, f32[256,256]{1,0:T(8,128)S(1)} %multiply_add_fusion.1, f32[256,256]{1,0:T(8,128)S(1)} %mul.143), kind=kOutput, calls=%fused_computation.1 | convolution fusion | flops 1610743808 | bytes 3670016 | tf_op jit(solution)/shard_map/kzp,pq->kzq/dot_general | solution.py:54
  4.7 2.4 %collective-permute-start = (f32[64,1,256]{2,0,1:T(8,128)S(1)}, f32[64,1,256]{2,0,1:T(8,128)S(1)}, u32[]{:S(2)}, u32[]{:S(2)}) collective-permute-start(f32[64,1,256]{2,0,1:T(8,128)S(1)} %get-tuple-element.8), channel_id=1, source_target_pairs={{0,1},{1,2},{2,3},{3,4},{4,5},{5,6},{6,7},{7,8},{8,9},{9,10},{10,1... | collective-permute-start | bytes 196616 | tf_op jit(solution)/shard_map/ppermute | solution.py:21
  7.1 1.3 collective-permute-start.1
  8.4 3.9 %collective-permute-done.1 = f32[64,1,256]{2,0,1:T(8,128)S(1)} collective-permute-done((f32[64,1,256]{2,0,1:T(8,128)S(1)}, f32[64,1,256]{2,0,1:T(8,128)S(1)}, u32[]{:S(2)}, u32[]{:S(2)}) %collective-permute-start.1) | collective-permute-done | bytes 65568 | tf_op jit(solution)/shard_map/ppermute | solution.py:23
  12.3 0.8 fusion.11
  13.2 1.8 %fusion.14 = f32[64,16,512]{2,0,1:T(8,128)S(1)} fusion(f32[64,16,256]{2,0,1:T(8,128)S(1)} %fusion.11, f32[256,256]{1,0:T(8,128)S(1)} %multiply_add_fusion.1, f32[256,256]{1,0:T(8,128)S(1)} %mul.143), kind=kOutput, calls=%fused_computation.30 | convolution fusion | flops 1610743808 | bytes 3670016 | tf_op jit(solution)/shard_map/kzp,pq->kzq/dot_general | solution.py:54
  15.2 4.8 %collective-permute-start.2 = (f32[64,1,256]{2,0,1:T(8,128)S(1)}, f32[64,1,256]{2,0,1:T(8,128)S(1)}, u32[]{:S(2)}, u32[]{:S(2)}) collective-permute-start(f32[64,1,256]{2,0,1:T(8,128)S(1)} %get-tuple-element.6), channel_id=1, source_target_pairs={{0,1},{1,2},{2,3},{3,4},{4,5},{5,6},{6,7},{7,8},{8,9},{9,10},{10,1... | collective-permute-start | bytes 196616 | tf_op jit(solution)/shard_map/ppermute | solution.py:21
  20.0 1.3 collective-permute-start.3
  21.4 1.8 %collective-permute-done.3 = f32[64,1,256]{2,0,1:T(8,128)S(1)} collective-permute-done((f32[64,1,256]{2,0,1:T(8,128)S(1)}, f32[64,1,256]{2,0,1:T(8,128)S(1)}, u32[]{:S(2)}, u32[]{:S(2)}) %collective-permute-start.3) | collective-permute-done | bytes 65568 | tf_op jit(solution)/shard_map/ppermute | solution.py:23
  23.2 0.3 fusion.7
  23.5 1.8 %fusion.13 = f32[64,16,512]{2,0,1:T(8,128)S(1)} fusion(f32[64,16,256]{2,0,1:T(8,128)S(1)} %fusion.7, f32[256,256]{1,0:T(8,128)S(1)} %multiply_add_fusion.1, f32[256,256]{1,0:T(8,128)S(1)} %mul.143), kind=kOutput, calls=%fused_computation.29 | convolution fusion | flops 1610743808 | bytes 3670016 | tf_op jit(solution)/shard_map/kzp,pq->kzq/dot_general | solution.py:54
  25.6 5.1 %collective-permute-start.4 = (f32[64,1,256]{2,0,1:T(8,128)S(1)}, f32[64,1,256]{2,0,1:T(8,128)S(1)}, u32[]{:S(2)}, u32[]{:S(2)}) collective-permute-start(f32[64,1,256]{2,0,1:T(8,128)S(1)} %get-tuple-element.4), channel_id=1, source_target_pairs={{0,1},{1,2},{2,3},{3,4},{4,5},{5,6},{6,7},{7,8},{8,9},{9,10},{10,1... | collective-permute-start | bytes 196616 | tf_op jit(solution)/shard_map/ppermute | solution.py:21
  30.7 1.3 collective-permute-start.5
  32.0 1.8 %collective-permute-done.5 = f32[64,1,256]{2,0,1:T(8,128)S(1)} collective-permute-done((f32[64,1,256]{2,0,1:T(8,128)S(1)}, f32[64,1,256]{2,0,1:T(8,128)S(1)}, u32[]{:S(2)}, u32[]{:S(2)}) %collective-permute-start.5) | collective-permute-done | bytes 65568 | tf_op jit(solution)/shard_map/ppermute | solution.py:23
  33.8 0.3 fusion.3
  34.1 1.0 convolution_bitcast_fusion.1
  35.1 45.9 %psum.14 = f32[64,64]{0,1:T(8,128)S(1)} all-reduce(f32[64,64]{0,1:T(8,128)S(1)} %convolution_bitcast_fusion.1), channel_id=1, replica_groups=mesh['sfc'=8,'sub'=4] {'sfc','sub'}, use_global_device_ids=true, to_apply=%region_0.1 | all-reduce | flops 4096 | bytes 32768 | tf_op jit(solution)/shard_map/psum | solution.py:68
  81.1 5.8 %cholesky.44 = f32[64,64]{1,0:T(8,128)S(1)} custom-call(f32[64,64]{1,0:T(8,128)S(1)} %fusion.19), custom_call_target="Cholesky" | custom-call | tf_op jit(solution)/shard_map/jit(cholesky)/cholesky | solution.py:69
  87.0 0.6 compare_reduce_fusion.1
  87.6 0.7 fusion.23
  88.3 4.9 %custom-call.6 = f32[1,64,64]{1,2,0:T(8,128)S(1)} custom-call(f32[1,64,64]{2,1,0:T(8,128)S(1)} %fusion.23), custom_call_target="InvertDiagBlocksLowerTriangular" | custom-call | tf_op jit(solution)/shard_map/triangular_solve/custom-call.0 | solution.py:73
  93.3 1.0 fusion.17
  94.3 1.0 fusion.44
  95.3 40.3 %psum.15 = f32[64,64]{0,1:T(8,128)S(1)} all-reduce(f32[64,64]{0,1:T(8,128)S(1)} %fusion.44), channel_id=1, replica_groups=mesh['sfc'=8,'sub'=4] {'sfc','sub'}, use_global_device_ids=true, to_apply=%region_3.6 | all-reduce | flops 4096 | bytes 32768 | tf_op jit(solution)/shard_map/psum | solution.py:68
  135.7 5.8 %cholesky.55 = f32[64,64]{1,0:T(8,128)S(1)} custom-call(f32[64,64]{1,0:T(8,128)S(1)} %fusion.16), custom_call_target="Cholesky" | custom-call | tf_op jit(solution)/shard_map/jit(cholesky)/cholesky | solution.py:69
  141.6 0.7 compare_reduce_fusion
  142.3 2.2 %convolution_multiply_fusion.1 = f32[64,64]{1,0:T(8,128)} fusion(f32[64,64]{1,0:T(8,128)S(1)} %cholesky.55, f32[64,64]{1,0:T(8,128)S(1)} %cholesky.44, pred[]{:T(512)} %compare_reduce_fusion, pred[]{:T(512)} %compare_reduce_fusion.1), kind=kOutput, calls=%fused_computation.2 | convolution fusion | flops 3174400 | bytes 49154 | tf_op jit(solution)/shard_map/dot_general | solution.py:87
  144.5 0.7 select_bitcast_fusion
  145.2 4.9 %custom-call.7 = f32[1,64,64]{1,2,0:T(8,128)S(1)} custom-call(f32[1,64,64]{2,1,0:T(8,128)S(1)} %select_bitcast_fusion), custom_call_target="InvertDiagBlocksLowerTriangular" | custom-call | tf_op jit(solution)/shard_map/triangular_solve/custom-call.0 | solution.py:73
  150.1 1.1 convolution_multiply_fusion
  151.2 1.3 copy.37
  (25 shorter events, 1.8 us)
Async XLA Ops:
  1.0 1.2 copy-start
  4.5 7.8 %copy-start.1 = (f32[16,256]{1,0:T(8,128)S(1)}, f32[16,256]{1,0:T(8,128)}, u32[]{:S(2)}) copy-start(f32[16,256]{1,0:T(8,128)} %param.6) | copy-start | bytes 49156
  4.7 3.7 %collective-permute-start = (f32[64,1,256]{2,0,1:T(8,128)S(1)}, f32[64,1,256]{2,0,1:T(8,128)S(1)}, u32[]{:S(2)}, u32[]{:S(2)}) collective-permute-start(f32[64,1,256]{2,0,1:T(8,128)S(1)} %get-tuple-element.8), channel_id=1, source_target_pairs={{0,1},{1,2},{2,3},{3,4},{4,5},{5,6},{6,7},{7,8},{8,9},{9,10},{10,1... | collective-permute-start | bytes 196616 | tf_op jit(solution)/shard_map/ppermute | solution.py:21
  7.1 5.2 %collective-permute-start.1 = (f32[64,1,256]{2,0,1:T(8,128)S(1)}, f32[64,1,256]{2,0,1:T(8,128)S(1)}, u32[]{:S(2)}, u32[]{:S(2)}) collective-permute-start(f32[64,1,256]{2,0,1:T(8,128)S(1)} %get-tuple-element.9), channel_id=1, source_target_pairs={{1,0},{2,1},{3,2},{4,3},{5,4},{6,5},{7,6},{8,7},{9,8},{10,9},{11,1... | collective-permute-start | bytes 196616 | tf_op jit(solution)/shard_map/ppermute | solution.py:23
  15.2 6.2 %collective-permute-start.2 = (f32[64,1,256]{2,0,1:T(8,128)S(1)}, f32[64,1,256]{2,0,1:T(8,128)S(1)}, u32[]{:S(2)}, u32[]{:S(2)}) collective-permute-start(f32[64,1,256]{2,0,1:T(8,128)S(1)} %get-tuple-element.6), channel_id=1, source_target_pairs={{0,1},{1,2},{2,3},{3,4},{4,5},{5,6},{6,7},{7,8},{8,9},{9,10},{10,1... | collective-permute-start | bytes 196616 | tf_op jit(solution)/shard_map/ppermute | solution.py:21
  20.0 3.1 %collective-permute-start.3 = (f32[64,1,256]{2,0,1:T(8,128)S(1)}, f32[64,1,256]{2,0,1:T(8,128)S(1)}, u32[]{:S(2)}, u32[]{:S(2)}) collective-permute-start(f32[64,1,256]{2,0,1:T(8,128)S(1)} %get-tuple-element.7), channel_id=1, source_target_pairs={{1,0},{2,1},{3,2},{4,3},{5,4},{6,5},{7,6},{8,7},{9,8},{10,9},{11,1... | collective-permute-start | bytes 196616 | tf_op jit(solution)/shard_map/ppermute | solution.py:23
  25.6 6.4 %collective-permute-start.4 = (f32[64,1,256]{2,0,1:T(8,128)S(1)}, f32[64,1,256]{2,0,1:T(8,128)S(1)}, u32[]{:S(2)}, u32[]{:S(2)}) collective-permute-start(f32[64,1,256]{2,0,1:T(8,128)S(1)} %get-tuple-element.4), channel_id=1, source_target_pairs={{0,1},{1,2},{2,3},{3,4},{4,5},{5,6},{6,7},{7,8},{8,9},{9,10},{10,1... | collective-permute-start | bytes 196616 | tf_op jit(solution)/shard_map/ppermute | solution.py:21
  30.7 3.1 %collective-permute-start.5 = (f32[64,1,256]{2,0,1:T(8,128)S(1)}, f32[64,1,256]{2,0,1:T(8,128)S(1)}, u32[]{:S(2)}, u32[]{:S(2)}) collective-permute-start(f32[64,1,256]{2,0,1:T(8,128)S(1)} %get-tuple-element.5), channel_id=1, source_target_pairs={{1,0},{2,1},{3,2},{4,3},{5,4},{6,5},{7,6},{8,7},{9,8},{10,9},{11,1... | collective-permute-start | bytes 196616 | tf_op jit(solution)/shard_map/ppermute | solution.py:23
where the time goes:
time: 153 us; the launch traced here: 152 us
  blocking collectives  86.2 us (56%)
  other arithmetic  26.6 us (17%)
  starting transfers between devices  16.2 us (11%)
  matrix products  12.2 us (8%)
  waiting for transfers between devices  7.62 us (5%)
  local copies, waits for them, and re-layouts  2.74 us (2%)
    psum x2, blocking collectives, whole_factor(): total = lax.psum(gram, ('sfc', 'sub'))  86.2 us
    another operation x6, other arithmetic, whole_factor(): return jnp.linalg.cholesky(total)  13.1 us
    ppermute x3, starting transfers between devices, with_halo(): lax.ppermute(tail, axis, [(i, (i + 1) % count) for i in range(ends)])  12.4 us
    another operation x4, other arithmetic, lower_solve(): return lax.linalg.triangular_solve(lower, block, left_side=True, lower=True)  11.1 us
    ppermute x3, waiting for transfers between devices, with_halo(): lax.ppermute(head, axis, [((i + 1) % count, i) for i in range(ends)])  7.61 us
    dot_general x3, matrix products, plane_products(): jnp.einsum('kzp,pq->kzq', field, table, precision=lax.Precision.HIGHEST)  5.98 us
    ppermute x3, starting transfers between devices, with_halo(): lax.ppermute(head, axis, [((i + 1) % count, i) for i in range(ends)])  3.88 us
  transfers between devices with their start and end apart: 6, of which 3 were waited for; matrix products, arithmetic and copies ran while one was open for 0% of the time, Pallas kernels for 0%

commit v1 on v0

--- a/solution.py
+++ b/solution.py
@@ -65,7 +65,7 @@
 
 def whole_factor(local):
     gram = jnp.dot(local, local.T, precision=lax.Precision.HIGHEST)
-    total = lax.psum(gram, ("sfc", "sub"))
+    total = jax.lax.psum(jax.lax.psum(gram, "sfc"), "sub")
     return jnp.linalg.cholesky(total)
 
 

time: 153 us -> 161 us (1.052)
  blocking collectives: 86.2 us -> 93.9 us
    psum x2 -> x4, blocking collectives: 86.2 us -> 93.9 us  [whole_factor(): total = jax.lax.psum(jax.lax.psum(gram, 'sfc'), 'sub')]
where the time goes in v1:
time: 161 us; the launch traced here: 160 us
  blocking collectives  93.9 us (58%)
  other arithmetic  26.6 us (17%)
  starting transfers between devices  16.2 us (10%)
  matrix products  12.2 us (8%)
  waiting for transfers between devices  7.62 us (5%)
  local copies, waits for them, and re-layouts  2.74 us (2%)
    psum x4, blocking collectives, whole_factor(): total = jax.lax.psum(jax.lax.psum(gram, 'sfc'), 'sub')  93.9 us
    another operation x6, other arithmetic, whole_factor(): return jnp.linalg.cholesky(total)  13.1 us
    ppermute x3, starting transfers between devices, with_halo(): lax.ppermute(tail, axis, [(i, (i + 1) % count) for i in range(ends)])  12.4 us
    another operation x4, other arithmetic, lower_solve(): return lax.linalg.triangular_solve(lower, block, left_side=True, lower=True)  11.1 us
    ppermute x3, waiting for transfers between devices, with_halo(): lax.ppermute(head, axis, [((i + 1) % count, i) for i in range(ends)])  7.61 us
    dot_general x3, matrix products, plane_products(): jnp.einsum('kzp,pq->kzq', field, table, precision=lax.Precision.HIGHEST)  5.98 us
    ppermute x3, starting transfers between devices, with_halo(): lax.ppermute(head, axis, [((i + 1) % count, i) for i in range(ends)])  3.88 us
  transfers between devices with their start and end apart: 6, of which 3 were waited for; matrix products, arithmetic and copies ran while one was open for 0% of the time, Pallas kernels for 0%

profile of v1, /device:TPU:0, one launch (start us, length us, event | category | flops | bytes accessed | tf_op | source)
XLA Modules:
  0.0 160.1 jit_solution(1731979829254288030)
XLA Ops:
  1.6 0.5 copy-done
  2.2 2.3 %convolution_bitcast_fusion = f32[64,16,512]{2,0,1:T(8,128)S(1)} fusion(f32[64,16,256]{2,1,0:T(8,128)S(1)} %copy-done, f32[256,256]{1,0:T(8,128)S(1)} %multiply_add_fusion.1, f32[256,256]{1,0:T(8,128)S(1)} %mul.143), kind=kOutput, calls=%fused_computation.1 | convolution fusion | flops 1610743808 | bytes 3670016 | tf_op jit(solution)/shard_map/kzp,pq->kzq/dot_general | solution.py:54
  4.7 2.4 %collective-permute-start = (f32[64,1,256]{2,0,1:T(8,128)S(1)}, f32[64,1,256]{2,0,1:T(8,128)S(1)}, u32[]{:S(2)}, u32[]{:S(2)}) collective-permute-start(f32[64,1,256]{2,0,1:T(8,128)S(1)} %get-tuple-element.8), channel_id=1, source_target_pairs={{0,1},{1,2},{2,3},{3,4},{4,5},{5,6},{6,7},{7,8},{8,9},{9,10},{10,1... | collective-permute-start | bytes 196616 | tf_op jit(solution)/shard_map/ppermute | solution.py:21
  7.1 1.3 collective-permute-start.1
  8.4 3.9 %collective-permute-done.1 = f32[64,1,256]{2,0,1:T(8,128)S(1)} collective-permute-done((f32[64,1,256]{2,0,1:T(8,128)S(1)}, f32[64,1,256]{2,0,1:T(8,128)S(1)}, u32[]{:S(2)}, u32[]{:S(2)}) %collective-permute-start.1) | collective-permute-done | bytes 65568 | tf_op jit(solution)/shard_map/ppermute | solution.py:23
  12.3 0.8 fusion.11
  13.2 1.8 %fusion.14 = f32[64,16,512]{2,0,1:T(8,128)S(1)} fusion(f32[64,16,256]{2,0,1:T(8,128)S(1)} %fusion.11, f32[256,256]{1,0:T(8,128)S(1)} %multiply_add_fusion.1, f32[256,256]{1,0:T(8,128)S(1)} %mul.143), kind=kOutput, calls=%fused_computation.30 | convolution fusion | flops 1610743808 | bytes 3670016 | tf_op jit(solution)/shard_map/kzp,pq->kzq/dot_general | solution.py:54
  15.2 4.8 %collective-permute-start.2 = (f32[64,1,256]{2,0,1:T(8,128)S(1)}, f32[64,1,256]{2,0,1:T(8,128)S(1)}, u32[]{:S(2)}, u32[]{:S(2)}) collective-permute-start(f32[64,1,256]{2,0,1:T(8,128)S(1)} %get-tuple-element.6), channel_id=1, source_target_pairs={{0,1},{1,2},{2,3},{3,4},{4,5},{5,6},{6,7},{7,8},{8,9},{9,10},{10,1... | collective-permute-start | bytes 196616 | tf_op jit(solution)/shard_map/ppermute | solution.py:21
  20.0 1.3 collective-permute-start.3
  21.4 1.8 %collective-permute-done.3 = f32[64,1,256]{2,0,1:T(8,128)S(1)} collective-permute-done((f32[64,1,256]{2,0,1:T(8,128)S(1)}, f32[64,1,256]{2,0,1:T(8,128)S(1)}, u32[]{:S(2)}, u32[]{:S(2)}) %collective-permute-start.3) | collective-permute-done | bytes 65568 | tf_op jit(solution)/shard_map/ppermute | solution.py:23
  23.5 1.8 %fusion.13 = f32[64,16,512]{2,0,1:T(8,128)S(1)} fusion(f32[64,16,256]{2,0,1:T(8,128)S(1)} %fusion.7, f32[256,256]{1,0:T(8,128)S(1)} %multiply_add_fusion.1, f32[256,256]{1,0:T(8,128)S(1)} %mul.143), kind=kOutput, calls=%fused_computation.29 | convolution fusion | flops 1610743808 | bytes 3670016 | tf_op jit(solution)/shard_map/kzp,pq->kzq/dot_general | solution.py:54
  25.6 5.1 %collective-permute-start.4 = (f32[64,1,256]{2,0,1:T(8,128)S(1)}, f32[64,1,256]{2,0,1:T(8,128)S(1)}, u32[]{:S(2)}, u32[]{:S(2)}) collective-permute-start(f32[64,1,256]{2,0,1:T(8,128)S(1)} %get-tuple-element.4), channel_id=1, source_target_pairs={{0,1},{1,2},{2,3},{3,4},{4,5},{5,6},{6,7},{7,8},{8,9},{9,10},{10,1... | collective-permute-start | bytes 196616 | tf_op jit(solution)/shard_map/ppermute | solution.py:21
  30.7 1.3 collective-permute-start.5
  32.0 1.8 %collective-permute-done.5 = f32[64,1,256]{2,0,1:T(8,128)S(1)} collective-permute-done((f32[64,1,256]{2,0,1:T(8,128)S(1)}, f32[64,1,256]{2,0,1:T(8,128)S(1)}, u32[]{:S(2)}, u32[]{:S(2)}) %collective-permute-start.5) | collective-permute-done | bytes 65568 | tf_op jit(solution)/shard_map/ppermute | solution.py:23
  34.1 1.0 convolution_bitcast_fusion.1
  35.1 40.1 %psum.28 = f32[64,64]{0,1:T(8,128)S(1)} all-reduce(f32[64,64]{0,1:T(8,128)S(1)} %convolution_bitcast_fusion.1), channel_id=1, replica_groups=mesh['sfc'=8,'sub'=4] {'sfc'}, use_global_device_ids=true, to_apply=%region_0.1 | all-reduce | flops 4096 | bytes 32768 | tf_op jit(solution)/shard_map/psum | solution.py:68
  75.3 10.4 %psum.29 = f32[64,64]{0,1:T(8,128)S(1)} all-reduce(f32[64,64]{0,1:T(8,128)S(1)} %psum.28), channel_id=1, replica_groups=mesh['sfc'=8,'sub'=4] {'sub'}, use_global_device_ids=true, to_apply=%region_1.2 | all-reduce | flops 4096 | bytes 32768 | tf_op jit(solution)/shard_map/psum | solution.py:68
  85.8 5.8 %cholesky.44 = f32[64,64]{1,0:T(8,128)S(1)} custom-call(f32[64,64]{1,0:T(8,128)S(1)} %fusion.19), custom_call_target="Cholesky" | custom-call | tf_op jit(solution)/shard_map/jit(cholesky)/cholesky | solution.py:69
  91.7 0.6 compare_reduce_fusion.1
  92.3 0.7 fusion.23
  93.0 4.9 %custom-call.6 = f32[1,64,64]{1,2,0:T(8,128)S(1)} custom-call(f32[1,64,64]{2,1,0:T(8,128)S(1)} %fusion.23), custom_call_target="InvertDiagBlocksLowerTriangular" | custom-call | tf_op jit(solution)/shard_map/triangular_solve/custom-call.0 | solution.py:73
  98.0 1.0 fusion.17
  99.0 1.0 fusion.44
  100.0 33.0 %psum.30 = f32[64,64]{0,1:T(8,128)S(1)} all-reduce(f32[64,64]{0,1:T(8,128)S(1)} %fusion.44), channel_id=1, replica_groups=mesh['sfc'=8,'sub'=4] {'sfc'}, use_global_device_ids=true, to_apply=%region_4.7 | all-reduce | flops 4096 | bytes 32768 | tf_op jit(solution)/shard_map/psum | solution.py:68
  133.0 10.3 %psum.31 = f32[64,64]{0,1:T(8,128)S(1)} all-reduce(f32[64,64]{0,1:T(8,128)S(1)} %psum.30), channel_id=1, replica_groups=mesh['sfc'=8,'sub'=4] {'sub'}, use_global_device_ids=true, to_apply=%region_5.8 | all-reduce | flops 4096 | bytes 32768 | tf_op jit(solution)/shard_map/psum | solution.py:68
  143.4 5.8 %cholesky.55 = f32[64,64]{1,0:T(8,128)S(1)} custom-call(f32[64,64]{1,0:T(8,128)S(1)} %fusion.16), custom_call_target="Cholesky" | custom-call | tf_op jit(solution)/shard_map/jit(cholesky)/cholesky | solution.py:69
  149.3 0.7 compare_reduce_fusion
  150.0 2.2 %convolution_multiply_fusion.1 = f32[64,64]{1,0:T(8,128)} fusion(f32[64,64]{1,0:T(8,128)S(1)} %cholesky.55, f32[64,64]{1,0:T(8,128)S(1)} %cholesky.44, pred[]{:T(512)} %compare_reduce_fusion, pred[]{:T(512)} %compare_reduce_fusion.1), kind=kOutput, calls=%fused_computation.2 | convolution fusion | flops 3174400 | bytes 49154 | tf_op jit(solution)/shard_map/dot_general | solution.py:87
  152.2 0.7 select_bitcast_fusion
  152.9 4.9 %custom-call.7 = f32[1,64,64]{1,2,0:T(8,128)S(1)} custom-call(f32[1,64,64]{2,1,0:T(8,128)S(1)} %select_bitcast_fusion), custom_call_target="InvertDiagBlocksLowerTriangular" | custom-call | tf_op jit(solution)/shard_map/triangular_solve/custom-call.0 | solution.py:73
  157.8 1.1 convolution_multiply_fusion
  158.8 1.3 copy.37
  (27 shorter events, 2.5 us)
Async XLA Ops:
  1.0 1.2 copy-start
  4.5 7.8 %copy-start.1 = (f32[16,256]{1,0:T(8,128)S(1)}, f32[16,256]{1,0:T(8,128)}, u32[]{:S(2)}) copy-start(f32[16,256]{1,0:T(8,128)} %param.6) | copy-start | bytes 49156
  4.7 3.7 %collective-permute-start = (f32[64,1,256]{2,0,1:T(8,128)S(1)}, f32[64,1,256]{2,0,1:T(8,128)S(1)}, u32[]{:S(2)}, u32[]{:S(2)}) collective-permute-start(f32[64,1,256]{2,0,1:T(8,128)S(1)} %get-tuple-element.8), channel_id=1, source_target_pairs={{0,1},{1,2},{2,3},{3,4},{4,5},{5,6},{6,7},{7,8},{8,9},{9,10},{10,1... | collective-permute-start | bytes 196616 | tf_op jit(solution)/shard_map/ppermute | solution.py:21
  7.1 5.2 %collective-permute-start.1 = (f32[64,1,256]{2,0,1:T(8,128)S(1)}, f32[64,1,256]{2,0,1:T(8,128)S(1)}, u32[]{:S(2)}, u32[]{:S(2)}) collective-permute-start(f32[64,1,256]{2,0,1:T(8,128)S(1)} %get-tuple-element.9), channel_id=1, source_target_pairs={{1,0},{2,1},{3,2},{4,3},{5,4},{6,5},{7,6},{8,7},{9,8},{10,9},{11,1... | collective-permute-start | bytes 196616 | tf_op jit(solution)/shard_map/ppermute | solution.py:23
  15.2 6.2 %collective-permute-start.2 = (f32[64,1,256]{2,0,1:T(8,128)S(1)}, f32[64,1,256]{2,0,1:T(8,128)S(1)}, u32[]{:S(2)}, u32[]{:S(2)}) collective-permute-start(f32[64,1,256]{2,0,1:T(8,128)S(1)} %get-tuple-element.6), channel_id=1, source_target_pairs={{0,1},{1,2},{2,3},{3,4},{4,5},{5,6},{6,7},{7,8},{8,9},{9,10},{10,1... | collective-permute-start | bytes 196616 | tf_op jit(solution)/shard_map/ppermute | solution.py:21
  20.0 3.1 %collective-permute-start.3 = (f32[64,1,256]{2,0,1:T(8,128)S(1)}, f32[64,1,256]{2,0,1:T(8,128)S(1)}, u32[]{:S(2)}, u32[]{:S(2)}) collective-permute-start(f32[64,1,256]{2,0,1:T(8,128)S(1)} %get-tuple-element.7), channel_id=1, source_target_pairs={{1,0},{2,1},{3,2},{4,3},{5,4},{6,5},{7,6},{8,7},{9,8},{10,9},{11,1... | collective-permute-start | bytes 196616 | tf_op jit(solution)/shard_map/ppermute | solution.py:23
  25.6 6.4 %collective-permute-start.4 = (f32[64,1,256]{2,0,1:T(8,128)S(1)}, f32[64,1,256]{2,0,1:T(8,128)S(1)}, u32[]{:S(2)}, u32[]{:S(2)}) collective-permute-start(f32[64,1,256]{2,0,1:T(8,128)S(1)} %get-tuple-element.4), channel_id=1, source_target_pairs={{0,1},{1,2},{2,3},{3,4},{4,5},{5,6},{6,7},{7,8},{8,9},{9,10},{10,1... | collective-permute-start | bytes 196616 | tf_op jit(solution)/shard_map/ppermute | solution.py:21
  30.7 3.1 %collective-permute-start.5 = (f32[64,1,256]{2,0,1:T(8,128)S(1)}, f32[64,1,256]{2,0,1:T(8,128)S(1)}, u32[]{:S(2)}, u32[]{:S(2)}) collective-permute-start(f32[64,1,256]{2,0,1:T(8,128)S(1)} %get-tuple-element.5), channel_id=1, source_target_pairs={{1,0},{2,1},{3,2},{4,3},{5,4},{6,5},{7,6},{8,7},{9,8},{10,9},{11,1... | collective-permute-start | bytes 196616 | tf_op jit(solution)/shard_map/ppermute | solution.py:23
